TPU v7x, 256 devices: a whole 4x4x8 slice. The times are simulated.
256 devices in a mesh: pts: 32 (over z, x_hi, core), bond: 8 (over x_lo, y).
Axes of the slice: x: 4 (x_hi: 2, x_lo: 2; x = x_hi * 2 + x_lo), y: 4, z: 8, core: 2. Of those that a mesh axis runs over, the one named last changes fastest.
Arguments:
- displacement: float32 [3, 128, 64, 256], P(None, 'pts', 'bond'), may hold values from -1.5 to 1.5
- velocity: float32 [3, 128, 64, 256], P(None, 'pts', 'bond'), may hold values from -6 to 6
- stiffness: float32 [128, 64, 256], P('pts', 'bond'), may hold values from 0.5 to 8
- offsets: int32 [256, 3], P('bond'), may hold values from -4 to 4, as said below
- intact: int32 [256, 128, 64, 256], P('bond', 'pts'), may hold values 0 or 1
Outputs:
- new_displacement: float32 [3, 128, 64, 256], P(None, 'pts', 'bond')
- new_velocity: float32 [3, 128, 64, 256], P(None, 'pts', 'bond')
Inputs may be any that keep to these rules, and one draw needn't show every extreme that they name: `offsets`: every nonzero lattice shift (a, b, c) with a * a + b * b + c * c <= 16, each exactly once, in an order drawn from the seed.
All inputs are finite; a program needn't handle non-finite values. No bound on the sum of `intact` on one device may be relied on, other than what follows from the above.
Results may differ from a plain program's by a relative error of at most 0.0003.
Values sent between devices are 32-bit elements; how exact they have to be, the bound alone decides.
A program may use at most 64 MiB of HBM per device.

v0:
```python
import math

import jax
import jax.numpy as jnp
from jax import lax
from jax.sharding import PartitionSpec as P

REACH = 4


SPACING = 6.0
FORCE_SCALE = 8.0
TIME_STEP = 0.5
LANE_PAD = 128


def laid_out(blocks, dim):
    blocks = jnp.moveaxis(blocks, 0, dim)
    shape = blocks.shape
    return blocks.reshape(*shape[:dim], shape[dim] * shape[dim + 1], *shape[dim + 2 :])


def from_everyone(array, axis):
    copies = jnp.broadcast_to(array, (lax.axis_size(axis), *array.shape))
    return lax.all_to_all(copies, axis, split_axis=0, concat_axis=0, tiled=True)


def gathered_copies(array, axis, dim):
    return laid_out(from_everyone(array, axis), dim)


def padded_2(block, sides, width):
    for axis, dim in sides:
        count = lax.axis_size(axis)
        forward = [(i, i + 1) for i in range(count - 1)]
        backward = [(target, source) for source, target in forward]
        low = lax.ppermute(
            lax.slice_in_dim(block, block.shape[dim] - width, None, axis=dim), axis, forward
        )
        high = lax.ppermute(lax.slice_in_dim(block, 0, width, axis=dim), axis, backward)
        block = jnp.concatenate([low, block, high], axis=dim)
    return block


def in_blocks(array, dim, count):
    shape = array.shape
    blocks = array.reshape(*shape[:dim], count, shape[dim] // count, *shape[dim + 1 :])
    return jnp.moveaxis(blocks, dim, 0)


def sum_at_owner(array, axis, dim):
    blocks = in_blocks(array, dim, lax.axis_size(axis))
    arrived = lax.all_to_all(blocks, axis, split_axis=0, concat_axis=0, tiled=True)
    return arrived.sum(axis=0)


def bond_forces(centre, padded, inside, shift, alive):
    shape = centre.shape
    lower = shift + REACH
    anchor = jnp.zeros((), jnp.int32)
    nearby = lax.dynamic_slice(padded, (anchor, lower[0], lower[1], lower[2]), shape)
    present = lax.dynamic_slice(inside, (lower[0], lower[1], lower[2]), shape[1:]) * alive.astype(
        centre.dtype
    )
    bond_vec = shift.astype(centre.dtype) * SPACING
    length = jnp.sqrt(jnp.sum(bond_vec * bond_vec))
    relative = bond_vec[:, None, None, None] + nearby[:3] - centre[:3]
    stretched = jnp.sqrt(jnp.sum(relative * relative, axis=0))
    strain = (stretched - length) / length
    coupling = 0.5 * (centre[3] + nearby[3]) * present / length
    return relative * (coupling * strain / stretched)


def on_device(displacement, velocity, stiffness, offsets, intact):
    slab_rows = displacement.shape[1]
    own_state = jnp.concatenate([displacement, stiffness[None]], axis=0)
    gathered = gathered_copies(own_state, "bond", 2)
    whole = padded_2(gathered, (("pts", 1),), REACH)
    centre = whole[:, REACH : REACH + slab_rows]
    upper_pad = LANE_PAD - REACH
    padded = jnp.pad(whole, ((0, 0), (0, 0), (REACH, REACH), (REACH, upper_pad)))
    first_row = lax.axis_index("pts") * slab_rows - REACH
    global_rows = first_row + jnp.arange(slab_rows + 2 * REACH, dtype=jnp.int32)
    valid_rows = ((global_rows >= 0) & (global_rows < slab_rows * lax.axis_size("pts"))).astype(
        jnp.float32
    )
    plane = jnp.pad(
        jnp.ones((whole.shape[2], whole.shape[3]), jnp.float32),
        ((REACH, REACH), (REACH, upper_pad)),
    )
    inside = valid_rows[:, None, None] * plane[None]
    group = math.gcd(offsets.shape[0], 8)
    turns = offsets.shape[0] // group
    shift_blocks = offsets.reshape((turns, group, 3))
    alive_blocks = intact.reshape((turns, group) + intact.shape[1:])
    batched = jax.vmap(bond_forces, in_axes=(None, None, None, 0, 0))

    def accumulate(total, pieces):
        shift_block, alive_block = pieces
        terms = batched(centre, padded, inside, shift_block, alive_block)
        return (total + jnp.sum(terms, axis=0), None)

    start_total = jnp.zeros((3,) + centre.shape[1:], jnp.float32)
    total = lax.scan(accumulate, start_total, (shift_blocks, alive_blocks))[0]
    force = sum_at_owner(total, "bond", 2)
    density = FORCE_SCALE * force
    new_velocity = velocity + TIME_STEP * density
    new_displacement = displacement + TIME_STEP * new_velocity
    return (new_displacement, new_velocity)


def solution(mesh):
    return jax.shard_map(
        on_device,
        mesh=mesh,
        in_specs=(
            P(None, "pts", "bond", None),
            P(None, "pts", "bond", None),
            P("pts", "bond", None),
            P("bond", None),
            P("bond", "pts", None, None),
        ),
        out_specs=(P(None, "pts", "bond", None), P(None, "pts", "bond", None)),
        check_vma=False,
    )
```

profile of v0, /device:TPU:129, one launch (start us, length us, event | category | flops | bytes accessed | tf_op | source)
XLA Modules:
  0.0 369.5 jit_solution(12437795321572588686)
XLA Ops:
  1.7 19.3 %all_to_all.10 = f32[8,4,4,8,256]{4,3,2,1,0:T(8,128)S(1)} all-to-all(f32[8,4,4,8,256]{4,3,2,1,0:T(8,128)S(1)} %broadcast_in_dim.10), channel_id=1, replica_groups=mesh['pts'=32,'bond'=8] {'bond'}, dimensions={0} | all-to-all | bytes 2097152 | tf_op jit(solution)/shard_map/all_to_all | solution.py:25
  30.8 21.8 %collective-permute-done.1 = f32[4,4,64,256]{3,2,1,0:T(8,128)S(1)} collective-permute-done((f32[4,4,64,256]{3,2,1,0:T(8,128)}, f32[4,4,64,256]{3,2,1,0:T(8,128)S(1)}, u32[]{:S(2)}, u32[]{:S(2)}) %collective-permute-start.1) | collective-permute-done | bytes 1048608 | tf_op jit(solution)/shard_map/ppermute | solution.py:40
  52.6 5.0 %select_maximum_fusion = f32[4,12,72,384]{3,2,1,0:T(8,128)} fusion(f32[4,4,64,256]{3,2,1,0:T(8,128)S(1)} %collective-permute-done.1, f32[4,4,64,256]{3,2,1,0:T(8,128)} %bitcast.45, f32[4,4,64,256]{3,2,1,0:T(8,128)S(1)} %collective-permute-done), kind=kLoop, calls=%fused_computation.37 | loop fusion | flops 19906560 | bytes 8454144 | tf_op jit(solution)/shard_map/concatenate | solution.py:41
  57.6 297.7 %while.19 = (s32[]{:T(128)}, f32[3,4,64,256]{3,2,1,0:T(8,128)}, s32[4,8,3]{1,0,2:T(4,128)S(1)}, f32[4,12,72,384]{3,2,1,0:T(8,128)}, f32[4,4,64,256]{3,2,1,0:T(8,...) while((s32[]{:T(128)}, f32[3,4,64,256]{3,2,1,0:T(8,128)}, ...), condition=%wide.region_4.5_spmd.clone, body=%wide.region_0.4_spmd.clone.sunk | while | flops 17830268 | bytes 78250400 | solution.py:104
  57.7 41.8 %while.20 = (s32[]{:T(128)}, f32[4,12,72,384]{3,2,1,0:T(8,128)}, s32[8,4]{0,1:T(4,128)S(1)}, f32[8,4,4,64,256]{4,3,2,1,0:T(8,128)}, s32[]{:T(128)}) while((s32[]{:T(128)}, f32[4,12,72,384]{3,2,1,0:T(8,128)}, s32[8,4]{0,1:T(4,128)S(1)}, f32[8,4,4,64,256]{4,3,2,1,0:T(8,128)}, s32[]{:T(128)}) %tuple.74), condition=%wide.while_cond, body=%wide.while_body.sunk | while | flops 2 | bytes 2098821 | solution.py:61
  63.5 4.6 %bitcast_dynamic-update-slice_fusion.4 = f32[8,4,4,64,256]{4,3,2,1,0:T(8,128)} fusion(f32[8,4,4,64,256]{4,3,2,1,0:T(8,128)} %get-tuple-element.302, s32[]{:T(128)S(6)} %copy.47, f32[4,12,72,384]{3,2,1,0:T(8,128)} %get-tuple-element.305, s32[]{:T(128)} %bitcast.73, s32[]{:T(128)} %bitcast.74, s32[]{:T(128)} %bitcast.75), kind=kLoop, calls=%fused_computation.1.clone.1 | loop fusion | bytes 2098692 | tf_op jit(solution)/shard_map/while/body/eval_jaxpr/vmap()/gather
  84.4 4.6 %bitcast_dynamic-update-slice_fusion.4 = f32[8,4,4,64,256]{4,3,2,1,0:T(8,128)} fusion(f32[8,4,4,64,256]{4,3,2,1,0:T(8,128)} %get-tuple-element.302, s32[]{:T(128)S(6)} %copy.47, f32[4,12,72,384]{3,2,1,0:T(8,128)} %get-tuple-element.305, s32[]{:T(128)} %bitcast.73, s32[]{:T(128)} %bitcast.74, s32[]{:T(128)} %bitcast.75), kind=kLoop, calls=%fused_computation.1.clone.1 | loop fusion | bytes 2098692 | tf_op jit(solution)/shard_map/while/body/eval_jaxpr/vmap()/gather
  89.6 4.6 %bitcast_dynamic-update-slice_fusion.4 = f32[8,4,4,64,256]{4,3,2,1,0:T(8,128)} fusion(f32[8,4,4,64,256]{4,3,2,1,0:T(8,128)} %get-tuple-element.302, s32[]{:T(128)S(6)} %copy.47, f32[4,12,72,384]{3,2,1,0:T(8,128)} %get-tuple-element.305, s32[]{:T(128)} %bitcast.73, s32[]{:T(128)} %bitcast.74, s32[]{:T(128)} %bitcast.75), kind=kLoop, calls=%fused_computation.1.clone.1 | loop fusion | bytes 2098692 | tf_op jit(solution)/shard_map/while/body/eval_jaxpr/vmap()/gather
  99.7 20.5 %while.21 = (s32[]{:T(128)}, f32[12,72,384]{2,1,0:T(8,128)S(1)}, s32[8,3]{0,1:T(4,128)S(1)}, f32[8,4,64,256]{3,2,1,0:T(8,128)S(1)}, s32[]{:T(128)}) while((s32[]{:T(128)}, f32[12,72,384]{2,1,0:T(8,128)S(1)}, s32[8,3]{0,1:T(4,128)S(1)}, f32[8,4,64,256]{3,2,1,0:T(8,128)S(1)}, s32[]{:T(128)}) %tuple.77), condition=%wide.while_cond.1, body=%wide.while_body.1.sunk | while | flops 2 | bytes 524425 | solution.py:62
  132.1 41.8 %while.20 = (s32[]{:T(128)}, f32[4,12,72,384]{3,2,1,0:T(8,128)}, s32[8,4]{0,1:T(4,128)S(1)}, f32[8,4,4,64,256]{4,3,2,1,0:T(8,128)}, s32[]{:T(128)}) while((s32[]{:T(128)}, f32[4,12,72,384]{3,2,1,0:T(8,128)}, s32[8,4]{0,1:T(4,128)S(1)}, f32[8,4,4,64,256]{4,3,2,1,0:T(8,128)}, s32[]{:T(128)}) %tuple.74), condition=%wide.while_cond, body=%wide.while_body.sunk | while | flops 2 | bytes 2098821 | solution.py:61
  137.9 4.6 %bitcast_dynamic-update-slice_fusion.4 = f32[8,4,4,64,256]{4,3,2,1,0:T(8,128)} fusion(f32[8,4,4,64,256]{4,3,2,1,0:T(8,128)} %get-tuple-element.302, s32[]{:T(128)S(6)} %copy.47, f32[4,12,72,384]{3,2,1,0:T(8,128)} %get-tuple-element.305, s32[]{:T(128)} %bitcast.73, s32[]{:T(128)} %bitcast.74, s32[]{:T(128)} %bitcast.75), kind=kLoop, calls=%fused_computation.1.clone.1 | loop fusion | bytes 2098692 | tf_op jit(solution)/shard_map/while/body/eval_jaxpr/vmap()/gather
  158.8 4.6 %bitcast_dynamic-update-slice_fusion.4 = f32[8,4,4,64,256]{4,3,2,1,0:T(8,128)} fusion(f32[8,4,4,64,256]{4,3,2,1,0:T(8,128)} %get-tuple-element.302, s32[]{:T(128)S(6)} %copy.47, f32[4,12,72,384]{3,2,1,0:T(8,128)} %get-tuple-element.305, s32[]{:T(128)} %bitcast.73, s32[]{:T(128)} %bitcast.74, s32[]{:T(128)} %bitcast.75), kind=kLoop, calls=%fused_computation.1.clone.1 | loop fusion | bytes 2098692 | tf_op jit(solution)/shard_map/while/body/eval_jaxpr/vmap()/gather
  164.1 4.6 %bitcast_dynamic-update-slice_fusion.4 = f32[8,4,4,64,256]{4,3,2,1,0:T(8,128)} fusion(f32[8,4,4,64,256]{4,3,2,1,0:T(8,128)} %get-tuple-element.302, s32[]{:T(128)S(6)} %copy.47, f32[4,12,72,384]{3,2,1,0:T(8,128)} %get-tuple-element.305, s32[]{:T(128)} %bitcast.73, s32[]{:T(128)} %bitcast.74, s32[]{:T(128)} %bitcast.75), kind=kLoop, calls=%fused_computation.1.clone.1 | loop fusion | bytes 2098692 | tf_op jit(solution)/shard_map/while/body/eval_jaxpr/vmap()/gather
  174.1 20.5 %while.21 = (s32[]{:T(128)}, f32[12,72,384]{2,1,0:T(8,128)S(1)}, s32[8,3]{0,1:T(4,128)S(1)}, f32[8,4,64,256]{3,2,1,0:T(8,128)S(1)}, s32[]{:T(128)}) while((s32[]{:T(128)}, f32[12,72,384]{2,1,0:T(8,128)S(1)}, s32[8,3]{0,1:T(4,128)S(1)}, f32[8,4,64,256]{3,2,1,0:T(8,128)S(1)}, s32[]{:T(128)}) %tuple.77), condition=%wide.while_cond.1, body=%wide.while_body.1.sunk | while | flops 2 | bytes 524425 | solution.py:62
  206.5 41.8 %while.20 = (s32[]{:T(128)}, f32[4,12,72,384]{3,2,1,0:T(8,128)}, s32[8,4]{0,1:T(4,128)S(1)}, f32[8,4,4,64,256]{4,3,2,1,0:T(8,128)}, s32[]{:T(128)}) while((s32[]{:T(128)}, f32[4,12,72,384]{3,2,1,0:T(8,128)}, s32[8,4]{0,1:T(4,128)S(1)}, f32[8,4,4,64,256]{4,3,2,1,0:T(8,128)}, s32[]{:T(128)}) %tuple.74), condition=%wide.while_cond, body=%wide.while_body.sunk | while | flops 2 | bytes 2098821 | solution.py:61
  212.4 4.6 %bitcast_dynamic-update-slice_fusion.4 = f32[8,4,4,64,256]{4,3,2,1,0:T(8,128)} fusion(f32[8,4,4,64,256]{4,3,2,1,0:T(8,128)} %get-tuple-element.302, s32[]{:T(128)S(6)} %copy.47, f32[4,12,72,384]{3,2,1,0:T(8,128)} %get-tuple-element.305, s32[]{:T(128)} %bitcast.73, s32[]{:T(128)} %bitcast.74, s32[]{:T(128)} %bitcast.75), kind=kLoop, calls=%fused_computation.1.clone.1 | loop fusion | bytes 2098692 | tf_op jit(solution)/shard_map/while/body/eval_jaxpr/vmap()/gather
  233.3 4.6 %bitcast_dynamic-update-slice_fusion.4 = f32[8,4,4,64,256]{4,3,2,1,0:T(8,128)} fusion(f32[8,4,4,64,256]{4,3,2,1,0:T(8,128)} %get-tuple-element.302, s32[]{:T(128)S(6)} %copy.47, f32[4,12,72,384]{3,2,1,0:T(8,128)} %get-tuple-element.305, s32[]{:T(128)} %bitcast.73, s32[]{:T(128)} %bitcast.74, s32[]{:T(128)} %bitcast.75), kind=kLoop, calls=%fused_computation.1.clone.1 | loop fusion | bytes 2098692 | tf_op jit(solution)/shard_map/while/body/eval_jaxpr/vmap()/gather
  238.5 4.6 %bitcast_dynamic-update-slice_fusion.4 = f32[8,4,4,64,256]{4,3,2,1,0:T(8,128)} fusion(f32[8,4,4,64,256]{4,3,2,1,0:T(8,128)} %get-tuple-element.302, s32[]{:T(128)S(6)} %copy.47, f32[4,12,72,384]{3,2,1,0:T(8,128)} %get-tuple-element.305, s32[]{:T(128)} %bitcast.73, s32[]{:T(128)} %bitcast.74, s32[]{:T(128)} %bitcast.75), kind=kLoop, calls=%fused_computation.1.clone.1 | loop fusion | bytes 2098692 | tf_op jit(solution)/shard_map/while/body/eval_jaxpr/vmap()/gather
  248.5 20.5 %while.21 = (s32[]{:T(128)}, f32[12,72,384]{2,1,0:T(8,128)S(1)}, s32[8,3]{0,1:T(4,128)S(1)}, f32[8,4,64,256]{3,2,1,0:T(8,128)S(1)}, s32[]{:T(128)}) while((s32[]{:T(128)}, f32[12,72,384]{2,1,0:T(8,128)S(1)}, s32[8,3]{0,1:T(4,128)S(1)}, f32[8,4,64,256]{3,2,1,0:T(8,128)S(1)}, s32[]{:T(128)}) %tuple.77), condition=%wide.while_cond.1, body=%wide.while_body.1.sunk | while | flops 2 | bytes 524425 | solution.py:62
  281.0 41.8 %while.20 = (s32[]{:T(128)}, f32[4,12,72,384]{3,2,1,0:T(8,128)}, s32[8,4]{0,1:T(4,128)S(1)}, f32[8,4,4,64,256]{4,3,2,1,0:T(8,128)}, s32[]{:T(128)}) while((s32[]{:T(128)}, f32[4,12,72,384]{3,2,1,0:T(8,128)}, s32[8,4]{0,1:T(4,128)S(1)}, f32[8,4,4,64,256]{4,3,2,1,0:T(8,128)}, s32[]{:T(128)}) %tuple.74), condition=%wide.while_cond, body=%wide.while_body.sunk | while | flops 2 | bytes 2098821 | solution.py:61
  286.8 4.6 %bitcast_dynamic-update-slice_fusion.4 = f32[8,4,4,64,256]{4,3,2,1,0:T(8,128)} fusion(f32[8,4,4,64,256]{4,3,2,1,0:T(8,128)} %get-tuple-element.302, s32[]{:T(128)S(6)} %copy.47, f32[4,12,72,384]{3,2,1,0:T(8,128)} %get-tuple-element.305, s32[]{:T(128)} %bitcast.73, s32[]{:T(128)} %bitcast.74, s32[]{:T(128)} %bitcast.75), kind=kLoop, calls=%fused_computation.1.clone.1 | loop fusion | bytes 2098692 | tf_op jit(solution)/shard_map/while/body/eval_jaxpr/vmap()/gather
  307.7 4.6 %bitcast_dynamic-update-slice_fusion.4 = f32[8,4,4,64,256]{4,3,2,1,0:T(8,128)} fusion(f32[8,4,4,64,256]{4,3,2,1,0:T(8,128)} %get-tuple-element.302, s32[]{:T(128)S(6)} %copy.47, f32[4,12,72,384]{3,2,1,0:T(8,128)} %get-tuple-element.305, s32[]{:T(128)} %bitcast.73, s32[]{:T(128)} %bitcast.74, s32[]{:T(128)} %bitcast.75), kind=kLoop, calls=%fused_computation.1.clone.1 | loop fusion | bytes 2098692 | tf_op jit(solution)/shard_map/while/body/eval_jaxpr/vmap()/gather
  323.0 20.5 %while.21 = (s32[]{:T(128)}, f32[12,72,384]{2,1,0:T(8,128)S(1)}, s32[8,3]{0,1:T(4,128)S(1)}, f32[8,4,64,256]{3,2,1,0:T(8,128)S(1)}, s32[]{:T(128)}) while((s32[]{:T(128)}, f32[12,72,384]{2,1,0:T(8,128)S(1)}, s32[8,3]{0,1:T(4,128)S(1)}, f32[8,4,64,256]{3,2,1,0:T(8,128)S(1)}, s32[]{:T(128)}) %tuple.77), condition=%wide.while_cond.1, body=%wide.while_body.1.sunk | while | flops 2 | bytes 524425 | solution.py:62
  356.6 11.3 %all_to_all.11 = f32[8,3,4,8,256]{4,3,2,1,0:T(8,128)S(1)} all-to-all(f32[8,3,4,8,256]{4,3,2,1,0:T(8,128)S(1)} %copy.17), channel_id=1, replica_groups=mesh['pts'=32,'bond'=8] {'bond'}, dimensions={0} | all-to-all | bytes 1572864 | tf_op jit(solution)/shard_map/all_to_all | solution.py:53
  (297 shorter events, 259.1 us)
Async XLA Ops:
  0.6 30.0 %copy-start.3 = (s32[32,3]{0,1:T(4,128)S(1)}, s32[32,3]{0,1:T(4,128)}, u32[]{:S(2)}) copy-start(s32[32,3]{0,1:T(4,128)} %param.10) | copy-start | bytes 1156
  22.0 30.5 %collective-permute-start.1 = (f32[4,4,64,256]{3,2,1,0:T(8,128)}, f32[4,4,64,256]{3,2,1,0:T(8,128)S(1)}, u32[]{:S(2)}, u32[]{:S(2)}) collective-permute-start(f32[4,4,64,256]{3,2,1,0:T(8,128)} %bitcast.45), channel_id=1, source_target_pairs={{8,0},{16,8},{24,16},{32,24},{40,32},{48,40},{56,48},{64,56},{72,6... | collective-permute-start | bytes 3145736 | tf_op jit(solution)/shard_map/ppermute | solution.py:40
  26.3 26.3 %collective-permute-start = (f32[4,4,64,256]{3,2,1,0:T(8,128)}, f32[4,4,64,256]{3,2,1,0:T(8,128)S(1)}, u32[]{:S(2)}, u32[]{:S(2)}) collective-permute-start(f32[4,4,64,256]{3,2,1,0:T(8,128)} %bitcast.45), channel_id=1, source_target_pairs={{0,8},{8,16},{16,24},{24,32},{32,40},{40,48},{48,56},{56,64},{64,7... | collective-permute-start | bytes 3145736 | tf_op jit(solution)/shard_map/ppermute | solution.py:37
  121.5 5.3 %copy-start = (f32[8,4,4,64,256]{4,3,2,1,0:T(8,128)S(1)}, f32[8,4,4,64,256]{4,3,2,1,0:T(8,128)}, u32[]{:S(2)}) copy-start(f32[8,4,4,64,256]{4,3,2,1,0:T(8,128)} %get-tuple-element.277) | copy-start | bytes 25165828 | tf_op jit(solution)/shard_map/while
  129.6 1.3 copy-start.1
  131.1 0.9 copy-start.2
  195.9 5.3 %copy-start = (f32[8,4,4,64,256]{4,3,2,1,0:T(8,128)S(1)}, f32[8,4,4,64,256]{4,3,2,1,0:T(8,128)}, u32[]{:S(2)}) copy-start(f32[8,4,4,64,256]{4,3,2,1,0:T(8,128)} %get-tuple-element.277) | copy-start | bytes 25165828 | tf_op jit(solution)/shard_map/while
  204.0 1.3 copy-start.1
  205.6 0.9 copy-start.2
  270.4 5.3 %copy-start = (f32[8,4,4,64,256]{4,3,2,1,0:T(8,128)S(1)}, f32[8,4,4,64,256]{4,3,2,1,0:T(8,128)}, u32[]{:S(2)}) copy-start(f32[8,4,4,64,256]{4,3,2,1,0:T(8,128)} %get-tuple-element.277) | copy-start | bytes 25165828 | tf_op jit(solution)/shard_map/while
  278.5 1.3 copy-start.1
  280.0 0.9 copy-start.2
  344.8 5.3 %copy-start = (f32[8,4,4,64,256]{4,3,2,1,0:T(8,128)S(1)}, f32[8,4,4,64,256]{4,3,2,1,0:T(8,128)}, u32[]{:S(2)}) copy-start(f32[8,4,4,64,256]{4,3,2,1,0:T(8,128)} %get-tuple-element.277) | copy-start | bytes 25165828 | tf_op jit(solution)/shard_map/while
  352.9 1.3 copy-start.1
  354.4 0.9 copy-start.2
where the time goes:
time: 375 us; the launch traced here: 370 us
  local copies, waits for them, and re-layouts  264 us (70%)
  other arithmetic  42.7 us (11%)
  blocking collectives  30.6 us (8%)
  waiting for transfers between devices  21.8 us (6%)
  starting transfers between devices  8.55 us (2%)
    gather x192, local copies, waits for them, and re-layouts  249 us
    ppermute x1, waiting for transfers between devices, padded_2(): lax.ppermute(lax.slice_in_dim(block, 0, width, axis=dim), axis, backward)  21.8 us
    all_to_all x1, blocking collectives, from_everyone(): return lax.all_to_all(copies, axis, split_axis=0, concat_axis=0, tiled=True)  19.3 us
    reduce_sum x4, other arithmetic, bond_forces(): stretched = jnp.sqrt(jnp.sum(relative * relative, axis=0))  17.1 us
    all_to_all x1, blocking collectives, sum_at_owner(): lax.all_to_all(blocks, axis, split_axis=0, concat_axis=0, tiled=True)  11.3 us
    mul x4, other arithmetic, bond_forces(): return relative * (coupling * strain / stretched)  11.1 us
  transfers between devices with their start and end apart: 2, of which 1 were waited for; matrix products, arithmetic and copies ran while one was open for 0% of the time, Pallas kernels for 0%

commit v1 on v0

v1 whole, which is shorter than its diff:
```python
import functools

import jax
import jax.numpy as jnp
from jax import lax
from jax.experimental import pallas as pl
from jax.experimental.pallas import tpu as pltpu
from jax.sharding import PartitionSpec as P

REACH = 4
SPACING = 6.0
FORCE_SCALE = 8.0
TIME_STEP = 0.5
SHIFTS = 2 * REACH + 1
LANES = 128
SUB = 8


def build_rows(table, load, slab, slab_rows, ytile, lane):
    for row in range(slab_rows):
        at = slab * slab_rows + row
        for comp in range(4):
            left, right = load(comp, row)
            if comp == 0:
                height = SPACING * (at - REACH - slab_rows // 2)
                left, right = left + height, right + height
            for shift in range(-REACH, REACH + 1):
                if shift == 0:
                    out = (left, right)
                elif shift > 0:
                    near = lane < LANES - shift
                    turned_l = pltpu.roll(left, LANES - shift, 1)
                    turned_r = pltpu.roll(right, LANES - shift, 1)
                    out = (jnp.where(near, turned_l, turned_r), jnp.where(near, turned_r, 0.0))
                else:
                    near = lane < -shift
                    turned_l = pltpu.roll(left, -shift, 1)
                    turned_r = pltpu.roll(right, -shift, 1)
                    out = (jnp.where(near, 0.0, turned_l), jnp.where(near, turned_l, turned_r))
                if comp == 2:
                    out = (out[0] + SPACING * shift, out[1] + SPACING * shift)
                base = ((shift + REACH) * 3 * slab_rows + at) * 2
                rows = pl.ds(pl.multiple_of(SUB + ytile * SUB, SUB), SUB)
                for half in range(2):
                    table[comp, base + half, rows, :] = out[half]


def clear_edges(table, slab_rows, ytiles):
    zero = jnp.zeros((SUB, LANES), jnp.float32)

    def body(index, carry):
        for comp in range(4):
            table[comp, index, pl.ds(0, SUB), :] = zero
            table[comp, index, pl.ds(SUB * (ytiles + 1), SUB), :] = zero
        return carry

    lax.fori_loop(0, SHIFTS * 3 * slab_rows * 2, body, 0)


def build_inside(inside, ytiles, lane):
    zero = jnp.zeros((SUB, LANES), jnp.float32)
    one = jnp.ones((SUB, LANES), jnp.float32)
    for index in range(SHIFTS + 1):
        shift = index - REACH
        for half in range(2):
            mask = zero
            if index < SHIFTS:
                z = lane + half * LANES + shift
                mask = jnp.where((z >= 0) & (z < 2 * LANES), one, zero)
            for tile in range(ytiles + 2):
                inner = 0 < tile <= ytiles
                inside[index, half, pl.ds(tile * SUB, SUB), :] = mask if inner else zero


def build_constants(constants, offsets):
    scale = FORCE_SCALE * TIME_STEP * 0.5
    zero = jnp.zeros((SUB, LANES), jnp.float32)

    def body(k, carry):
        a, b, c = offsets[k, 0], offsets[k, 1], offsets[k, 2]
        square = zero + (SPACING * SPACING) * (a * a + b * b + c * c).astype(jnp.float32)
        constants[k, 0] = scale / square
        constants[k, 1] = scale / jnp.sqrt(square)
        return carry

    lax.fori_loop(0, offsets.shape[0], body, 0)


def tile_force(table, inside, constants, offsets, alive, ytile, half, slab_rows, total_rows, first):
    count = offsets.shape[0]
    middle = SHIFTS // 2 * 3 * slab_rows
    here = pl.ds(pl.multiple_of(SUB + ytile * SUB, SUB), SUB)
    centre = [
        [table[comp, (middle + slab_rows + row) * 2 + half, here, :] for comp in range(4)]
        for row in range(slab_rows)
    ]

    def body(k, total):
        a, b, c = offsets[k, 0], offsets[k, 1], offsets[k, 2]
        start = ((c + REACH) * 3 * slab_rows + slab_rows + a) * 2 + half
        rows = pl.ds(SUB + ytile * SUB + b, SUB)
        rise = SPACING * b.astype(jnp.float32)
        c0, c1 = constants[k, 0], constants[k, 1]
        out = []
        for row in range(slab_rows):
            at = first + row + a
            valid = (at >= 0) & (at < total_rows)
            present = inside[jnp.where(valid, c + REACH, SHIFTS), half, rows, :]
            x, y, z, micro = (table[comp, start + 2 * row, rows, :] for comp in range(4))
            px, py, pz, pmicro = centre[row]
            rx = x - px
            ry = (y + rise) - py
            rz = z - pz
            inverse = lax.rsqrt(rx * rx + ry * ry + rz * rz)
            mask = alive(k, row, half).astype(jnp.float32)
            weight = (pmicro * present + micro) * mask * (c0 - c1 * inverse)
            fx, fy, fz = total[row]
            out.append((fx + weight * rx, fy + weight * ry, fz + weight * rz))
        return tuple(out)

    zero = jnp.zeros((SUB, LANES), jnp.float32)
    start_total = tuple((zero, zero, zero) for _ in range(slab_rows))
    return lax.fori_loop(0, count, body, start_total, unroll=2)


def force_kernel(
    pts, slab_rows, ytiles, offsets, low, mid, high, intact, out, table, inside, constants, mask, sem
):
    def fetch(tile):
        return pltpu.make_async_copy(
            intact.at[:, :, pl.ds(tile * SUB, SUB), :], mask.at[tile], sem.at[tile]
        )

    for tile in range(ytiles):
        fetch(tile).start()
    lane = lax.broadcasted_iota(jnp.int32, (SUB, LANES), 1)
    build_constants(constants, offsets)
    build_inside(inside, ytiles, lane)
    clear_edges(table, slab_rows, ytiles)

    def build(tile, carry):
        for slab, source in enumerate((low, mid, high)):

            def load(comp, row, source=source):
                return (
                    source[tile, comp, row, :, pl.ds(0, LANES)],
                    source[tile, comp, row, :, pl.ds(LANES, LANES)],
                )

            build_rows(table, load, slab, slab_rows, tile, lane)
        return carry

    lax.fori_loop(0, ytiles, build, 0)
    first = lax.axis_index("pts") * slab_rows

    def work(tile, carry):
        fetch(tile).wait()
        for half in range(2):

            def alive(k, row, half):
                return mask[tile, k, row, :, pl.ds(half * LANES, LANES)]

            total = tile_force(
                table, inside, constants, offsets, alive, tile, half,
                slab_rows, slab_rows * pts, first,
            )
            for row in range(slab_rows):
                for comp in range(3):
                    out[tile, comp, row, :, pl.ds(half * LANES, LANES)] = total[row][comp]
        return carry

    lax.fori_loop(0, ytiles, work, 0)


def on_device(pts, displacement, velocity, stiffness, offsets, intact):
    slab_rows = displacement.shape[1]
    count, _, ny, nz = intact.shape
    ytiles = ny // SUB
    own = jnp.concatenate([displacement, stiffness[None]], axis=0)
    copies = jnp.broadcast_to(own, (ytiles, *own.shape))
    mid = lax.all_to_all(copies, "bond", split_axis=0, concat_axis=0, tiled=True)
    up = [(i, i + 1) for i in range(pts - 1)]
    low = lax.ppermute(mid, "pts", up)
    high = lax.ppermute(mid, "pts", [(j, i) for i, j in up])
    vmem = pl.BlockSpec(memory_space=pltpu.VMEM)
    force = pl.pallas_call(
        functools.partial(force_kernel, pts, slab_rows, ytiles),
        out_shape=jax.ShapeDtypeStruct((ytiles, 3, slab_rows, SUB, nz), jnp.float32),
        in_specs=[
            pl.BlockSpec(memory_space=pltpu.SMEM), vmem, vmem, vmem,
            pl.BlockSpec(memory_space=pl.ANY),
        ],
        out_specs=vmem,
        scratch_shapes=[
            pltpu.VMEM((4, SHIFTS * 3 * slab_rows * 2, (ytiles + 2) * SUB, LANES), jnp.float32),
            pltpu.VMEM((SHIFTS + 1, 2, (ytiles + 2) * SUB, LANES), jnp.float32),
            pltpu.VMEM((count, 2, SUB, LANES), jnp.float32),
            pltpu.VMEM((ytiles, count, slab_rows, SUB, nz), jnp.int32),
            pltpu.SemaphoreType.DMA((ytiles,)),
        ],
        compiler_params=pltpu.CompilerParams(vmem_limit_bytes=60 << 20),
        name="bond_forces",
    )(offsets, low, mid, high, intact)
    arrived = lax.all_to_all(force, "bond", split_axis=0, concat_axis=0, tiled=True)
    new_velocity = velocity + arrived.sum(axis=0)
    new_displacement = displacement + TIME_STEP * new_velocity
    return new_displacement, new_velocity


def solution(mesh):
    return jax.shard_map(
        functools.partial(on_device, mesh.shape["pts"]),
        mesh=mesh,
        in_specs=(
            P(None, "pts", "bond", None),
            P(None, "pts", "bond", None),
            P("pts", "bond", None),
            P("bond", None),
            P("bond", "pts", None, None),
        ),
        out_specs=(P(None, "pts", "bond", None), P(None, "pts", "bond", None)),
        check_vma=False,
    )
```

time: 375 us -> 91.7 us (0.24); the launches traced: 370 us -> 90.9 us
  local copies, waits for them, and re-layouts: 264 us -> 3.44 us
  other arithmetic: 42.7 us -> 1.67 us
  Pallas kernels: 0 us -> 24.4 us
    gather x192 -> x0, local copies, waits for them, and re-layouts: 249 us -> none
    pallas_call x0 -> x1, Pallas kernels: none -> 24.4 us  [on_device(): pl.pallas_call(functools.partial(force_kernel, pts, slab_rows, ytiles), o...]
    reduce_sum x13 -> x1, other arithmetic: 22.2 us -> 0.05 us  [on_device(): new_velocity = velocity + arrived.sum(axis=0)]
    mul x12 -> x0, other arithmetic: 11.7 us -> none  [the longest x4 11.1 us: bond_forces(): return relative * (coupling * strain / stretched)]
    concatenate x10 -> x1, other arithmetic: 6.03 us -> 0.92 us  [on_device(): own = jnp.concatenate([displacement, stiffness[None]], axis=0)]
    slice x4 -> x0, local copies, waits for them, and re-layouts: 4.83 us -> none  [bond_forces(): relative = bond_vec[:, None, None, None] + nearby[:3] - centre[:3]]
    add x4 -> x0, local copies, waits for them, and re-layouts: 3.89 us -> none  [bond_forces(): coupling = 0.5 * (centre[3] + nearby[3]) * present / length]
  transfers between devices with their start and end apart: 2 -> 2, of which waited for: 1 -> 1; matrix products, arithmetic and copies ran while one was open for 0% -> 2% of each run, Pallas kernels for 0% -> 0%
where the time goes in v1:
time: 91.7 us; the launch traced here: 90.9 us
  blocking collectives  31.7 us (35%)
  Pallas kernels  24.4 us (27%)
  waiting for transfers between devices  20.4 us (22%)
  starting transfers between devices  8.55 us (9%)
  local copies, waits for them, and re-layouts  3.44 us (4%)
  other arithmetic  1.67 us (2%)
    pallas_call x1, Pallas kernels, on_device(): pl.pallas_call(functools.partial(force_kernel, pts, slab_rows, ytiles), o...  24.4 us
    ppermute x1, waiting for transfers between devices, on_device(): high = lax.ppermute(mid, 'pts', [(j, i) for i, j in up])  20.4 us
    all_to_all x1, blocking collectives, on_device(): lax.all_to_all(copies, 'bond', split_axis=0, concat_axis=0, tiled=True)  19.4 us
    all_to_all x1, blocking collectives, on_device(): lax.all_to_all(force, 'bond', split_axis=0, concat_axis=0, tiled=True)  12.3 us
    ppermute x1, starting transfers between devices, on_device(): high = lax.ppermute(mid, 'pts', [(j, i) for i, j in up])  4.29 us
    ppermute x1, starting transfers between devices, on_device(): low = lax.ppermute(mid, 'pts', up)  4.26 us
    unnamed x11, local copies, waits for them, and re-layouts  3.33 us
  transfers between devices with their start and end apart: 2, of which 1 were waited for; matrix products, arithmetic and copies ran while one was open for 2% of the time, Pallas kernels for 0%

profile of v1, /device:TPU:129, one launch (start us, length us, event | category | flops | bytes accessed | tf_op | source)
XLA Modules:
  0.0 90.9 jit_solution(17289549653557881973)
XLA Ops:
  0.6 0.9 %pad_maximum_fusion = f32[4,4,8,256]{3,2,1,0:T(8,128)S(1)} fusion(f32[1,4,8,256]{3,2,1,0:T(8,128)} %bitcast.1, f32[3,4,8,256]{3,2,1,0:T(8,128)} %param.5), kind=kLoop, calls=%fused_computation | loop fusion | flops 32768 | bytes 262144 | tf_op jit(solution)/shard_map/concatenate | solution.py:179
  1.6 0.1 broadcast_in_dim.7
  1.7 0.0 copy-start.3
  1.7 0.0 copy-start.4
  1.7 19.4 %all_to_all.10.mid = f32[8,4,4,8,256]{4,3,2,1,0:T(8,128)S(1)} all-to-all(f32[8,4,4,8,256]{4,3,2,1,0:T(8,128)S(1)} %broadcast_in_dim.7), channel_id=1, replica_groups=mesh['pts'=32,'bond'=8] {'bond'}, dimensions={0} | all-to-all | bytes 2097152 | tf_op jit(solution)/shard_map/all_to_all | solution.py:181
  21.1 0.0 copy-start
  21.1 4.3 %collective-permute-start.1 = (f32[8,4,4,8,256]{4,3,2,1,0:T(8,128)S(1)}, f32[8,4,4,8,256]{4,3,2,1,0:T(8,128)S(1)}, u32[]{:S(2)}, u32[]{:S(2)}) collective-permute-start(f32[8,4,4,8,256]{4,3,2,1,0:T(8,128)S(1)} %all_to_all.10.mid), channel_id=1, source_target_pairs={{8,0},{16,8},{24,16},{32,24},{40,32},{48,40},{56,48},{64,56},{72,6... | collective-permute-start | bytes 3145736 | tf_op jit(solution)/shard_map/ppermute | solution.py:184
  25.4 4.3 %collective-permute-start = (f32[8,4,4,8,256]{4,3,2,1,0:T(8,128)S(1)}, f32[8,4,4,8,256]{4,3,2,1,0:T(8,128)S(1)}, u32[]{:S(2)}, u32[]{:S(2)}) collective-permute-start(f32[8,4,4,8,256]{4,3,2,1,0:T(8,128)S(1)} %all_to_all.10.mid), channel_id=1, source_target_pairs={{0,8},{8,16},{16,24},{24,32},{32,40},{40,48},{48,56},{56,64},{64,7... | collective-permute-start | bytes 3145736 | tf_op jit(solution)/shard_map/ppermute | solution.py:183
  29.6 1.4 %copy.7.offsets = s32[32,3]{1,0:T(8,128)} copy(s32[32,3]{0,1:T(4,128)} %param.8) | data formatting | bytes 768 | tf_op args[3]
  31.0 20.4 %collective-permute-done.1.high = f32[8,4,4,8,256]{4,3,2,1,0:T(8,128)S(1)} collective-permute-done((f32[8,4,4,8,256]{4,3,2,1,0:T(8,128)S(1)}, f32[8,4,4,8,256]{4,3,2,1,0:T(8,128)S(1)}, u32[]{:S(2)}, u32[]{:S(2)}) %collective-permute-start.1) | collective-permute-done | bytes 1048608 | tf_op jit(solution)/shard_map/ppermute | solution.py:184
  51.4 0.0 copy-start.1
  51.4 0.0 collective-permute-done.low
  51.4 0.0 copy-done
  51.4 1.0 %copy-done.1 = f32[8,4,4,8,256]{4,3,2,1,0:T(8,128)} copy-done((f32[8,4,4,8,256]{4,3,2,1,0:T(8,128)}, f32[8,4,4,8,256]{4,3,2,1,0:T(8,128)S(1)}, u32[]{:S(2)}) %copy-start.1) | copy-done | bytes 1048600
  52.4 0.0 copy-start.2
  52.4 1.0 %copy-done.2 = f32[8,4,4,8,256]{4,3,2,1,0:T(8,128)} copy-done((f32[8,4,4,8,256]{4,3,2,1,0:T(8,128)}, f32[8,4,4,8,256]{4,3,2,1,0:T(8,128)S(1)}, u32[]{:S(2)}) %copy-start.2) | copy-done | bytes 1048600
  53.4 24.4 %bond_forces.1 = f32[8,3,4,8,256]{4,3,2,1,0:T(8,128)} custom-call(s32[32,3]{1,0:T(8,128)} %copy.7.offsets, f32[8,4,4,8,256]{4,3,2,1,0:T(8,128)} %copy-done.2, f32[8,4,4,8,256]{4,3,2,1,0:T(8,128)} %copy-done, f32[8,4,4,8,256]{4,3,2,1,0:T(8,128)} %copy-done.1, s32[32,4,64,256]{3,2,1,0:T(8,128)} %intact.1), custom_call_target="tpu_custom_call" | custom-call | tf_op jit(solution)/shard_map/bond_forces/pallas_call | solution.py:186
  77.8 12.3 %all_to_all.11 = f32[8,3,4,8,256]{4,3,2,1,0:T(8,128)S(1)} all-to-all(f32[8,3,4,8,256]{4,3,2,1,0:T(8,128)} %bond_forces.1), channel_id=1, replica_groups=mesh['pts'=32,'bond'=8] {'bond'}, dimensions={0} | all-to-all | bytes 1572864 | tf_op jit(solution)/shard_map/all_to_all | solution.py:204
  90.1 0.1 reduce_sum.9
  90.2 0.0 copy-done.3
  90.2 0.0 copy-done.4
  90.2 0.7 multiply_add_fusion
Async XLA Ops:
  1.7 88.5 %copy-start.3 = (f32[3,4,8,256]{3,2,1,0:T(8,128)S(1)}, f32[3,4,8,256]{3,2,1,0:T(8,128)}, u32[]{:S(2)}) copy-start(f32[3,4,8,256]{3,2,1,0:T(8,128)} %param.5) | copy-start | bytes 294916
  1.7 88.5 %copy-start.4 = (f32[3,4,8,256]{3,2,1,0:T(8,128)S(1)}, f32[3,4,8,256]{3,2,1,0:T(8,128)}, u32[]{:S(2)}) copy-start(f32[3,4,8,256]{3,2,1,0:T(8,128)} %param.6) | copy-start | bytes 294916
  21.1 30.3 %copy-start = (f32[8,4,4,8,256]{4,3,2,1,0:T(8,128)}, f32[8,4,4,8,256]{4,3,2,1,0:T(8,128)S(1)}, u32[]{:S(2)}) copy-start(f32[8,4,4,8,256]{4,3,2,1,0:T(8,128)S(1)} %all_to_all.10.mid) | copy-start | bytes 3145732
  21.1 30.3 %collective-permute-start.1 = (f32[8,4,4,8,256]{4,3,2,1,0:T(8,128)S(1)}, f32[8,4,4,8,256]{4,3,2,1,0:T(8,128)S(1)}, u32[]{:S(2)}, u32[]{:S(2)}) collective-permute-start(f32[8,4,4,8,256]{4,3,2,1,0:T(8,128)S(1)} %all_to_all.10.mid), channel_id=1, source_target_pairs={{8,0},{16,8},{24,16},{32,24},{40,32},{48,40},{56,48},{64,56},{72,6... | collective-permute-start | bytes 3145736 | tf_op jit(solution)/shard_map/ppermute | solution.py:184
  25.4 26.0 %collective-permute-start = (f32[8,4,4,8,256]{4,3,2,1,0:T(8,128)S(1)}, f32[8,4,4,8,256]{4,3,2,1,0:T(8,128)S(1)}, u32[]{:S(2)}, u32[]{:S(2)}) collective-permute-start(f32[8,4,4,8,256]{4,3,2,1,0:T(8,128)S(1)} %all_to_all.10.mid), channel_id=1, source_target_pairs={{0,8},{8,16},{16,24},{24,32},{32,40},{40,48},{48,56},{56,64},{64,7... | collective-permute-start | bytes 3145736 | tf_op jit(solution)/shard_map/ppermute | solution.py:183
  51.4 1.0 %copy-start.1 = (f32[8,4,4,8,256]{4,3,2,1,0:T(8,128)}, f32[8,4,4,8,256]{4,3,2,1,0:T(8,128)S(1)}, u32[]{:S(2)}) copy-start(f32[8,4,4,8,256]{4,3,2,1,0:T(8,128)S(1)} %collective-permute-done.1.high) | copy-start | bytes 3145732
  52.4 1.0 %copy-start.2 = (f32[8,4,4,8,256]{4,3,2,1,0:T(8,128)}, f32[8,4,4,8,256]{4,3,2,1,0:T(8,128)S(1)}, u32[]{:S(2)}) copy-start(f32[8,4,4,8,256]{4,3,2,1,0:T(8,128)S(1)} %collective-permute-done.low) | copy-start | bytes 3145732

commit v2 on v0

v2 whole, which is shorter than its diff:
```python
import functools

import jax
import jax.numpy as jnp
from jax import lax
from jax.experimental import pallas as pl
from jax.experimental.pallas import tpu as pltpu
from jax.sharding import PartitionSpec as P

REACH = 4
SPACING = 6.0
FORCE_SCALE = 8.0
TIME_STEP = 0.5
SHIFTS = 2 * REACH + 1
LANES = 128
SUB = 8
RING = 4
MESH = pl.DeviceIdType.MESH


def needed_rows(slab, shift, rows):
    if slab == 1:
        return 0, rows
    depth = max(d for d in range(rows + 1) if d * d + shift * shift <= REACH * REACH)
    return (rows - depth, rows) if slab == 0 else (0, depth)


def build_piece(table, pieces, slab, ytile, rows, lane):
    here = pl.ds(pl.multiple_of(SUB + ytile * SUB, SUB), SUB)
    for comp in range(4):
        left = pieces[slab, ytile, comp, :, :, pl.ds(0, LANES)]
        right = pieces[slab, ytile, comp, :, :, pl.ds(LANES, LANES)]
        if comp == 0:
            step = lax.broadcasted_iota(jnp.int32, left.shape, 0).astype(jnp.float32)
            height = SPACING * (step + float((slab - 1) * rows - rows // 2))
            left, right = left + height, right + height
        for shift in range(-REACH, REACH + 1):
            lo, hi = needed_rows(slab, shift, rows)
            if hi == lo:
                continue
            l, r = left[lo:hi], right[lo:hi]
            near = lane[lo:hi]
            if shift == 0:
                out = (l, r)
            elif shift > 0:
                near = near < LANES - shift
                l = pltpu.roll(l, LANES - shift, 2)
                r = pltpu.roll(r, LANES - shift, 2)
                out = (jnp.where(near, l, r), jnp.where(near, r, 0.0))
            else:
                near = near < -shift
                l = pltpu.roll(l, -shift, 2)
                r = pltpu.roll(r, -shift, 2)
                out = (jnp.where(near, 0.0, l), jnp.where(near, l, r))
            if comp == 2:
                out = (out[0] + SPACING * shift, out[1] + SPACING * shift)
            for half in range(2):
                at = (shift + REACH) * 2 + half
                table[comp, at, pl.ds(slab * rows + lo, hi - lo), here, :] = out[half]


def build_frame(table, rows, ytiles, first, total_rows):
    shape = (3 * rows, SUB, LANES)
    zero = jnp.zeros(shape, jnp.float32)
    lane = lax.broadcasted_iota(jnp.int32, shape, 2)
    row = lax.broadcasted_iota(jnp.int32, shape, 0) + (first - rows)
    row_in = (row >= 0) & (row < total_rows)

    def body(at, carry):
        z = lane + at % 2 * LANES + (at // 2 - REACH)
        mask = jnp.where(row_in & (z >= 0) & (z < 2 * LANES), 1.0, 0.0)
        for comp in range(5):
            table[comp, at, :, pl.ds(0, SUB), :] = zero
            table[comp, at, :, pl.ds(SUB * (ytiles + 1), SUB), :] = zero
        for tile in range(ytiles):
            table[4, at, :, pl.ds(SUB * (tile + 1), SUB), :] = mask
        return carry

    lax.fori_loop(0, 2 * SHIFTS, body, 0)


def build_constants(constants, offsets, count):
    scale = FORCE_SCALE * TIME_STEP * 0.5
    zero = jnp.zeros((SUB, LANES), jnp.float32)

    def body(k, carry):
        a, b, c = offsets[0, k], offsets[1, k], offsets[2, k]
        square = zero + (SPACING * SPACING) * (a * a + b * b + c * c).astype(jnp.float32)
        constants[k, 0] = scale / square
        constants[k, 1] = scale / jnp.sqrt(square)
        constants[k, 2] = zero + SPACING * b.astype(jnp.float32)
        return carry

    lax.fori_loop(0, count, body, 0)


def tile_force(table, constants, offsets, mask, ytile, half, rows, count):
    here = pl.ds(pl.multiple_of(SUB + ytile * SUB, SUB), SUB)
    px, py, pz, pmicro = (
        table[comp, REACH * 2 + half, pl.ds(rows, rows), here, :] for comp in range(4)
    )

    def body(k, total):
        a, b, c = offsets[0, k], offsets[1, k], offsets[2, k]
        at = (c + REACH) * 2 + half
        slab = pl.ds(rows + a, rows)
        there = pl.ds(SUB + ytile * SUB + b, SUB)
        x, y, z, micro, inside = (table[comp, at, slab, there, :] for comp in range(5))
        rx = x - px
        ry = (y + constants[k, 2]) - py
        rz = z - pz
        inverse = lax.rsqrt(rx * rx + ry * ry + rz * rz)
        alive = mask[ytile, k, :, :, pl.ds(half * LANES, LANES)].astype(jnp.float32)
        weight = (pmicro * inside + micro) * alive * (constants[k, 0] - constants[k, 1] * inverse)
        fx, fy, fz = total
        return fx + weight * rx, fy + weight * ry, fz + weight * rz

    zero = jnp.zeros((rows, SUB, LANES), jnp.float32)
    return lax.fori_loop(0, count, body, (zero, zero, zero), unroll=4)


def step_kernel(
    pts, rows, ytiles, count,
    offsets, displacement, stiffness, intact, out,
    table, constants, pieces, mask, partial, arrived,
    load_sem, mask_sem, send_sem, mid_sem, near_sem, far_sem, back_send, back_sem,
):
    p, b = lax.axis_index("pts"), lax.axis_index("bond")
    pair, y = b // RING, b % RING
    core = p % 2
    near_p = p + 1 - 2 * core
    far_p = p - 1 + 2 * core
    has_far = (far_p >= 0) & (far_p < pts)
    near_slot, far_slot = 2 - 2 * core, 2 * core

    def place(flip, turn):
        return (pair + flip) % 2 * RING + (y + turn) % RING

    def fetch(tile):
        return pltpu.make_async_copy(
            intact.at[:, :, pl.ds(tile * SUB, SUB), :], mask.at[tile], mask_sem.at[tile]
        )

    loads = [
        pltpu.make_async_copy(displacement, pieces.at[1, b, pl.ds(0, 3)], load_sem.at[0]),
        pltpu.make_async_copy(stiffness, pieces.at[1, b, 3], load_sem.at[1]),
    ]
    for load in loads:
        load.start()
    barrier = pltpu.get_barrier_semaphore()
    for other in range(1, 2 * RING):
        pl.semaphore_signal(
            barrier, inc=1, device_id=(p, place(other // RING, other % RING)), device_id_type=MESH
        )
    pl.semaphore_signal(barrier, inc=1, device_id=(near_p, b), device_id_type=MESH)

    @pl.when(has_far)
    def _():
        pl.semaphore_signal(
            barrier, inc=1, device_id=(far_p, place(1, 0)), device_id_type=MESH
        )

    @pl.when(has_far)
    def _():
        pl.semaphore_wait(barrier, 2 * RING + 1)

    @pl.when(jnp.logical_not(has_far))
    def _():
        pl.semaphore_wait(barrier, 2 * RING)

    for load in loads:
        load.wait()

    used = []

    def copy_of(source_slot, slot, origin, device, sems):
        index = len(used)
        return pltpu.make_async_remote_copy(
            src_ref=pieces.at[source_slot, origin],
            dst_ref=pieces.at[slot, origin],
            send_sem=send_sem.at[index],
            recv_sem=sems.at[origin],
            device_id=device,
            device_id_type=MESH,
        )

    def along(origin, flip, turn):
        copy = copy_of(1, 1, origin, (p, place(flip, turn)), mid_sem)
        used.append((copy, False))
        copy.start()

    def to_near(origin):
        copy = copy_of(1, far_slot, origin, (near_p, b), near_sem)
        used.append((copy, False))
        copy.start()

    def to_far(origin):
        copy = copy_of(1, near_slot, origin, (far_p, place(1, 0)), far_sem)
        used.append((copy, True))

        @pl.when(has_far)
        def _():
            copy.start()

    def far_on(origin):
        copy = copy_of(far_slot, far_slot, origin, (p, place(1, 0)), far_sem)
        used.append((copy, True))

        @pl.when(has_far)
        def _():
            arrival(far_slot, origin, far_sem).wait_recv()
            copy.start()

    def arrival(slot, origin, sems):
        return pltpu.make_async_remote_copy(
            src_ref=pieces.at[slot, origin],
            dst_ref=pieces.at[slot, origin],
            send_sem=send_sem.at[0],
            recv_sem=sems.at[origin],
            device_id=(near_p, b),
            device_id_type=MESH,
        )

    def await_mid(flip, turn):
        origin = place(flip, turn)
        arrival(1, origin, mid_sem).wait_recv()
        return origin

    lane = lax.broadcasted_iota(jnp.int32, (rows, SUB, LANES), 2)

    def build(slab, tiles):
        build_piece(table, pieces, slab, tiles, rows, lane)

    own = place(0, 0)
    along(own, 0, 1)
    to_far(own)
    along(own, 1, 0)
    along(own, 0, -1)
    to_near(own)
    for tile in range(ytiles):
        fetch((b + 1 + tile) % ytiles).start()
    build_constants(constants, offsets, count)
    build_frame(table, rows, ytiles, p * rows, pts * rows)

    @pl.when(jnp.logical_not(has_far))
    def _():
        def clear(tile, carry):
            pieces[far_slot, tile] = jnp.zeros(pieces.shape[2:], jnp.float32)
            return carry

        lax.fori_loop(0, ytiles, clear, 0)

    origin = await_mid(0, -1)
    to_far(origin)
    along(origin, 0, 1)
    to_near(origin)
    origin = await_mid(0, 1)
    to_far(origin)
    to_near(origin)
    origin = await_mid(1, 0)
    along(origin, 0, -1)
    along(origin, 0, 1)
    to_near(origin)
    far_on(place(1, 0))

    def build_mid(flip, start, number):
        def body(index, carry):
            build(1, place(flip, start + index))
            return carry

        lax.fori_loop(0, number, body, 0)

    def build_side(lower, origin):
        @pl.when(lower)
        def _():
            build(0, origin)

        @pl.when(jnp.logical_not(lower))
        def _():
            build(2, origin)

    def build_near(flip, start, number):
        def body(index, carry):
            origin = place(flip, start + index)
            arrival(near_slot, origin, near_sem).wait_recv()
            build_side(core == 1, origin)
            return carry

        lax.fori_loop(0, number, body, 0)

    def build_far(flip, start, number, waited):
        def body(index, carry):
            origin = place(flip, start + index)
            if not waited:

                @pl.when(has_far)
                def _():
                    arrival(far_slot, origin, far_sem).wait_recv()

            build_side(core == 0, origin)
            return carry

        lax.fori_loop(0, number, body, 0)

    build_mid(0, -1, 3)
    build_near(0, -1, 3)
    far_on(place(1, -1))
    far_on(place(1, 1))
    origin = await_mid(0, 2)
    to_far(origin)
    to_near(origin)
    origin = await_mid(1, 1)
    along(origin, 0, -1)
    to_near(origin)
    origin = await_mid(1, -1)
    to_near(origin)
    build_mid(0, 2, 1)
    build_mid(1, -1, 3)
    build_far(1, -1, 3, True)
    origin = await_mid(1, 2)
    to_near(origin)
    far_on(place(1, 2))
    build_near(1, -1, 3)
    build_near(0, 2, 1)
    build_mid(1, 2, 1)
    build_far(1, 2, 1, True)
    build_near(1, 2, 1)
    build_far(0, -1, 4, False)

    def back(step, tile):
        return pltpu.make_async_remote_copy(
            src_ref=partial.at[tile],
            dst_ref=arrived.at[step],
            send_sem=back_send.at[step],
            recv_sem=back_sem.at[step],
            device_id=(p, tile),
            device_id_type=MESH,
        )

    def target(step):
        return place(1 - step // RING, step + 1)

    def work(step, carry):
        tile = target(step)
        fetch(tile).wait()
        for half in range(2):
            total = tile_force(table, constants, offsets, mask, tile, half, rows, count)
            for comp in range(3):
                partial[tile, comp, :, :, pl.ds(half * LANES, LANES)] = total[comp]
            if half == 0:

                @pl.when(step > 0)
                def _():
                    back(step - 1, target(step - 1)).start()

        return carry

    lax.fori_loop(0, ytiles, work, 0)
    for copy, far in used:
        if far:

            @pl.when(has_far)
            def _(copy=copy):
                copy.wait_send()
        else:
            copy.wait_send()
    total = partial[b]
    for step in range(ytiles - 1):
        back(step, target(step)).wait_send()
        back(step, target(step)).wait_recv()
        total = total + arrived[step]
    out[...] = total


def on_device(pts, displacement, velocity, stiffness, offsets, intact):
    rows = displacement.shape[1]
    count, _, ny, nz = intact.shape
    ytiles = ny // SUB
    anywhere = pl.BlockSpec(memory_space=pl.ANY)
    change = pl.pallas_call(
        functools.partial(step_kernel, pts, rows, ytiles, count),
        out_shape=jax.ShapeDtypeStruct((3, rows, SUB, nz), jnp.float32),
        in_specs=[pl.BlockSpec(memory_space=pltpu.SMEM), anywhere, anywhere, anywhere],
        out_specs=pl.BlockSpec(memory_space=pltpu.VMEM),
        scratch_shapes=[
            pltpu.VMEM((5, SHIFTS * 2, 3 * rows, (ytiles + 2) * SUB, LANES), jnp.float32),
            pltpu.VMEM((count, 3, SUB, LANES), jnp.float32),
            pltpu.VMEM((3, ytiles, 4, rows, SUB, nz), jnp.float32),
            pltpu.VMEM((ytiles, count, rows, SUB, nz), jnp.int32),
            pltpu.VMEM((ytiles, 3, rows, SUB, nz), jnp.float32),
            pltpu.VMEM((ytiles - 1, 3, rows, SUB, nz), jnp.float32),
            pltpu.SemaphoreType.DMA((2,)),
            pltpu.SemaphoreType.DMA((ytiles,)),
            pltpu.SemaphoreType.DMA((24,)),
            pltpu.SemaphoreType.DMA((ytiles,)),
            pltpu.SemaphoreType.DMA((ytiles,)),
            pltpu.SemaphoreType.DMA((ytiles,)),
            pltpu.SemaphoreType.DMA((ytiles,)),
            pltpu.SemaphoreType.DMA((ytiles,)),
        ],
        compiler_params=pltpu.CompilerParams(
            vmem_limit_bytes=67043328, collective_id=0, has_side_effects=True
        ),
        name="bond_step",
    )(offsets.T, displacement, stiffness, intact)
    new_velocity = velocity + change
    new_displacement = displacement + TIME_STEP * new_velocity
    return new_displacement, new_velocity


def solution(mesh):
    return jax.shard_map(
        functools.partial(on_device, mesh.shape["pts"]),
        mesh=mesh,
        in_specs=(
            P(None, "pts", "bond", None),
            P(None, "pts", "bond", None),
            P("pts", "bond", None),
            P("bond", None),
            P("bond", "pts", None, None),
        ),
        out_specs=(P(None, "pts", "bond", None), P(None, "pts", "bond", None)),
        check_vma=False,
    )
```

time: 375 us -> 45.6 us (0.12); the launches traced: 370 us -> 45.4 us
  local copies, waits for them, and re-layouts: 264 us -> 0 us
  Pallas kernels: 0 us -> 43.1 us
  other arithmetic: 42.7 us -> 1.68 us
  blocking collectives: 30.6 us -> 0 us
  waiting for transfers between devices: 21.8 us -> 0 us
  starting transfers between devices: 8.55 us -> 0 us
    gather x192 -> x0, local copies, waits for them, and re-layouts: 249 us -> none
    pallas_call x0 -> x1, Pallas kernels: none -> 43.1 us  [on_device(): pl.pallas_call(functools.partial(step_kernel, pts, rows, ytiles, count),...]
    all_to_all x2 -> x0, blocking collectives: 30.6 us -> none  [the longest x1 19.3 us: from_everyone(): return lax.all_to_all(copies, axis, split_axis=0, concat_axis=0, tiled=True)]
    reduce_sum x13 -> x0, other arithmetic: 22.2 us -> none  [the longest x4 17.1 us: bond_forces(): stretched = jnp.sqrt(jnp.sum(relative * relative, axis=0))]
    ppermute x2 -> x0, waiting for transfers between devices: 21.8 us -> none  [the longest x1 21.8 us: padded_2(): lax.ppermute(lax.slice_in_dim(block, 0, width, axis=dim), axis, backward)]
    mul x12 -> x0, other arithmetic: 11.7 us -> none  [the longest x4 11.1 us: bond_forces(): return relative * (coupling * strain / stretched)]
    ppermute x2 -> x0, starting transfers between devices: 8.55 us -> none  [the longest x1 4.29 us: padded_2(): lax.ppermute(lax.slice_in_dim(block, 0, width, axis=dim), axis, backward)]
    concatenate x10 -> x0, other arithmetic: 6.03 us -> none  [the longest x1 5.01 us: padded_2(): block = jnp.concatenate([low, block, high], axis=dim)]
  transfers between devices with their start and end apart: 2 -> 0, of which waited for: 1 -> 0; matrix products, arithmetic and copies ran while one was open for 0% -> 0% of each run, Pallas kernels for 0% -> 0%
where the time goes in v2:
time: 45.6 us; the launch traced here: 45.4 us
  Pallas kernels  43.1 us (95%)
  other arithmetic  1.68 us (4%)
  between operations  0.64 us (1%)
    pallas_call x1, Pallas kernels, on_device(): pl.pallas_call(functools.partial(step_kernel, pts, rows, ytiles, count),...  43.1 us
    add x1, other arithmetic, on_device(): new_displacement = displacement + TIME_STEP * new_velocity  1.68 us

profile of v2, /device:TPU:129, one launch (start us, length us, event | category | flops | bytes accessed | tf_op | source)
XLA Modules:
  0.0 45.4 jit_solution(11097780774794409197)
XLA Ops:
  0.6 43.1 %bond_step.1 = f32[3,4,8,256]{3,2,1,0:T(8,128)} custom-call(s32[3,32]{1,0:T(4,128)} %bitcast.1, f32[3,4,8,256]{3,2,1,0:T(8,128)} %displacement.1, f32[4,8,256]{2,1,0:T(8,128)} %stiffness.1, s32[32,4,64,256]{3,2,1,0:T(8,128)} %intact.1), custom_call_target="tpu_custom_call" | custom-call | tf_op jit(solution)/shard_map/bond_step/pallas_call | solution.py:380
  43.7 1.7 %multiply_add_fusion = (f32[3,4,8,256]{3,2,1,0:T(8,128)}, f32[3,4,8,256]{3,2,1,0:T(8,128)}) fusion(f32[3,4,8,256]{3,2,1,0:T(8,128)} %displacement.1, f32[3,4,8,256]{3,2,1,0:T(8,128)} %param.6, f32[3,4,8,256]{3,2,1,0:T(8,128)} %bond_step.1), kind=kLoop, calls=%fused_computation | loop fusion | flops 73728 | bytes 491520 | tf_op jit(solution)/shard_map/add | solution.py:407

commit v3 on v2

--- a/solution.py
+++ b/solution.py
@@ -173,57 +173,66 @@
 
     used = []
 
-    def copy_of(source_slot, slot, origin, device, sems):
-        index = len(used)
-        return pltpu.make_async_remote_copy(
-            src_ref=pieces.at[source_slot, origin],
-            dst_ref=pieces.at[slot, origin],
-            send_sem=send_sem.at[index],
-            recv_sem=sems.at[origin],
+    def copy_of(source_slot, slot, origin, comps, device, sem):
+        copy = pltpu.make_async_remote_copy(
+            src_ref=pieces.at[source_slot, origin, comps],
+            dst_ref=pieces.at[slot, origin, comps],
+            send_sem=send_sem.at[len(used)],
+            recv_sem=sem,
             device_id=device,
             device_id_type=MESH,
         )
-
-    def along(origin, flip, turn):
-        copy = copy_of(1, 1, origin, (p, place(flip, turn)), mid_sem)
+        return copy
+
+    def comps_of(part):
+        return pl.ds(2 * part, 2)
+
+    def along(origin, part, flip, turn):
+        copy = copy_of(
+            1, 1, origin, comps_of(part), (p, place(flip, turn)), mid_sem.at[origin, part]
+        )
         used.append((copy, False))
         copy.start()
 
     def to_near(origin):
-        copy = copy_of(1, far_slot, origin, (near_p, b), near_sem)
+        copy = copy_of(1, far_slot, origin, pl.ds(0, 4), (near_p, b), near_sem.at[origin])
         used.append((copy, False))
         copy.start()
 
-    def to_far(origin):
-        copy = copy_of(1, near_slot, origin, (far_p, place(1, 0)), far_sem)
+    def to_far(origin, part):
+        copy = copy_of(
+            1, near_slot, origin, comps_of(part), (far_p, place(1, 0)), far_sem.at[origin, part]
+        )
         used.append((copy, True))
 
         @pl.when(has_far)
         def _():
             copy.start()
 
-    def far_on(origin):
-        copy = copy_of(far_slot, far_slot, origin, (p, place(1, 0)), far_sem)
+    def far_on(origin, part):
+        copy = copy_of(
+            far_slot, far_slot, origin, comps_of(part), (p, place(1, 0)), far_sem.at[origin, part]
+        )
         used.append((copy, True))
 
         @pl.when(has_far)
         def _():
-            arrival(far_slot, origin, far_sem).wait_recv()
+            arrival(far_slot, origin, comps_of(part), far_sem.at[origin, part]).wait_recv()
             copy.start()
 
-    def arrival(slot, origin, sems):
+    def arrival(slot, origin, comps, sem):
         return pltpu.make_async_remote_copy(
-            src_ref=pieces.at[slot, origin],
-            dst_ref=pieces.at[slot, origin],
+            src_ref=pieces.at[slot, origin, comps],
+            dst_ref=pieces.at[slot, origin, comps],
             send_sem=send_sem.at[0],
-            recv_sem=sems.at[origin],
+            recv_sem=sem,
             device_id=(near_p, b),
             device_id_type=MESH,
         )
 
-    def await_mid(flip, turn):
+    def await_mid(flip, turn, part):
         origin = place(flip, turn)
-        arrival(1, origin, mid_sem).wait_recv()
+        arrival(1, origin, comps_of(part), mid_sem.at[origin, part]).wait_recv()
         return origin
 
     lane = lax.broadcasted_iota(jnp.int32, (rows, SUB, LANES), 2)
@@ -232,10 +241,11 @@
         build_piece(table, pieces, slab, tiles, rows, lane)
 
     own = place(0, 0)
-    along(own, 0, 1)
-    to_far(own)
-    along(own, 1, 0)
-    along(own, 0, -1)
+    for part in range(2):
+        along(own, part, 0, 1)
+        along(own, part, 0, -1)
+        to_far(own, part)
+        along(own, part, 1, 0)
     to_near(own)
     for tile in range(ytiles):
         fetch((b + 1 + tile) % ytiles).start()
@@ -250,18 +260,19 @@
 
         lax.fori_loop(0, ytiles, clear, 0)
 
-    origin = await_mid(0, -1)
-    to_far(origin)
-    along(origin, 0, 1)
-    to_near(origin)
-    origin = await_mid(0, 1)
-    to_far(origin)
-    to_near(origin)
-    origin = await_mid(1, 0)
-    along(origin, 0, -1)
-    along(origin, 0, 1)
-    to_near(origin)
-    far_on(place(1, 0))
+    for part in range(2):
+        origin = await_mid(0, -1, part)
+        along(origin, part, 0, 1)
+        to_far(origin, part)
+        origin = await_mid(0, 1, part)
+        to_far(origin, part)
+        origin = await_mid(1, 0, part)
+        along(origin, part, 0, -1)
+        along(origin, part, 0, 1)
+    for origin in (place(0, -1), place(0, 1), place(1, 0)):
+        to_near(origin)
+    for part in range(2):
+        far_on(place(1, 0), part)
 
     def build_mid(flip, start, number):
         def body(index, carry):
@@ -282,7 +293,7 @@
     def build_near(flip, start, number):
         def body(index, carry):
             origin = place(flip, start + index)
-            arrival(near_slot, origin, near_sem).wait_recv()
+            arrival(near_slot, origin, pl.ds(0, 4), near_sem.at[origin]).wait_recv()
             build_side(core == 1, origin)
             return carry
 
@@ -295,7 +306,10 @@
 
                 @pl.when(has_far)
                 def _():
-                    arrival(far_slot, origin, far_sem).wait_recv()
+                    for part in range(2):
+                        arrival(
+                            far_slot, origin, comps_of(part), far_sem.at[origin, part]
+                        ).wait_recv()
 
             build_side(core == 0, origin)
             return carry
@@ -304,58 +318,89 @@
 
     build_mid(0, -1, 3)
     build_near(0, -1, 3)
-    far_on(place(1, -1))
-    far_on(place(1, 1))
-    origin = await_mid(0, 2)
-    to_far(origin)
-    to_near(origin)
-    origin = await_mid(1, 1)
-    along(origin, 0, -1)
-    to_near(origin)
-    origin = await_mid(1, -1)
-    to_near(origin)
+    for part in range(2):
+        origin = await_mid(0, 2, part)
+        to_far(origin, part)
+        far_on(place(1, -1), part)
+    to_near(place(0, 2))
+    for part in range(2):
+        origin = await_mid(1, 1, part)
+        along(origin, part, 0, -1)
+    to_near(place(1, 1))
+    for part in range(2):
+        await_mid(1, -1, part)
+    to_near(place(1, -1))
+    for part in range(2):
+        far_on(place(1, 1), part)
     build_mid(0, 2, 1)
     build_mid(1, -1, 3)
     build_far(1, -1, 3, True)
-    origin = await_mid(1, 2)
-    to_near(origin)
-    far_on(place(1, 2))
     build_near(1, -1, 3)
     build_near(0, 2, 1)
+    for part in range(2):
+        await_mid(1, 2, part)
+    to_near(place(1, 2))
+    for part in range(2):
+        far_on(place(1, 2), part)
     build_mid(1, 2, 1)
     build_far(1, 2, 1, True)
     build_near(1, 2, 1)
-    build_far(0, -1, 4, False)
-
-    def back(step, tile):
+
+    def back(step, slot, tile):
         return pltpu.make_async_remote_copy(
             src_ref=partial.at[tile],
-            dst_ref=arrived.at[step],
+            dst_ref=arrived.at[slot],
             send_sem=back_send.at[step],
-            recv_sem=back_sem.at[step],
+            recv_sem=back_sem.at[slot],
             device_id=(p, tile),
             device_id_type=MESH,
         )
 
-    def target(step):
-        return place(1 - step // RING, step + 1)
-
-    def work(step, carry):
-        tile = target(step)
+    across = 1 - pair
+    last = 2 * RING - 1
+
+    def early(step):
+        return across * last + (1 - 2 * across) * ((step + y) % (RING - 1))
+
+    border = RING - 1 + across
+
+    def work(tile, between):
         fetch(tile).wait()
         for half in range(2):
             total = tile_force(table, constants, offsets, mask, tile, half, rows, count)
             for comp in range(3):
                 partial[tile, comp, :, :, pl.ds(half * LANES, LANES)] = total[comp]
             if half == 0:
-
-                @pl.when(step > 0)
-                def _():
-                    back(step - 1, target(step - 1)).start()
-
+                between()
+
+    def work_early(step, carry):
+        def between():
+            @pl.when(step > 0)
+            def _():
+                back(step - 1, y, early(step - 1)).start()
+
+        work(early(step), between)
         return carry
 
-    lax.fori_loop(0, ytiles, work, 0)
+    def work_late(step, carry):
+        def between():
+            @pl.when(step == RING)
+            def _():
+                back(RING - 1, y, border).start()
+
+            @pl.when(step > RING)
+            def _():
+                back(step - 1, step - 1, place(0, step)).start()
+
+        work(place(0, step + 1), between)
+        return carry
+
+    lax.fori_loop(0, RING - 1, work_early, 0)
+    build_far(0, -1, 1, False)
+    back(RING - 2, y, early(RING - 2)).start()
+    build_far(0, 0, 3, False)
+    work(border, lambda: None)
+    lax.fori_loop(RING, 2 * RING, work_late, 0)
     for copy, far in used:
         if far:
 
@@ -365,10 +410,10 @@
         else:
             copy.wait_send()
     total = partial[b]
-    for step in range(ytiles - 1):
-        back(step, target(step)).wait_send()
-        back(step, target(step)).wait_recv()
-        total = total + arrived[step]
+    for slot in range(ytiles - 1):
+        back(slot, slot, border).wait_send()
+        back(slot, slot, border).wait_recv()
+        total = total + arrived[slot]
     out[...] = total
 
 
@@ -391,15 +436,15 @@
             pltpu.VMEM((ytiles - 1, 3, rows, SUB, nz), jnp.float32),
             pltpu.SemaphoreType.DMA((2,)),
             pltpu.SemaphoreType.DMA((ytiles,)),
-            pltpu.SemaphoreType.DMA((24,)),
+            pltpu.SemaphoreType.DMA((40,)),
+            pltpu.SemaphoreType.DMA((ytiles, 2)),
             pltpu.SemaphoreType.DMA((ytiles,)),
-            pltpu.SemaphoreType.DMA((ytiles,)),
-            pltpu.SemaphoreType.DMA((ytiles,)),
+            pltpu.SemaphoreType.DMA((ytiles, 2)),
             pltpu.SemaphoreType.DMA((ytiles,)),
             pltpu.SemaphoreType.DMA((ytiles,)),
         ],
         compiler_params=pltpu.CompilerParams(
-            vmem_limit_bytes=67043328, collective_id=0, has_side_effects=True
+            vmem_limit_bytes=59 << 20, collective_id=0, has_side_effects=True
         ),
         name="bond_step",
     )(offsets.T, displacement, stiffness, intact)

time: 45.6 us -> 43.9 us (0.963); the launches traced: 45.4 us -> 43.2 us
  Pallas kernels: 43.1 us -> 40.9 us
    pallas_call x1, Pallas kernels: 43.1 us -> 40.9 us  [on_device(): pl.pallas_call(functools.partial(step_kernel, pts, rows, ytiles, count),...]
where the time goes in v3:
time: 43.9 us; the launch traced here: 43.2 us
  Pallas kernels  40.9 us (93%)
  other arithmetic  1.59 us (4%)
  between operations  0.67 us (2%)
    pallas_call x1, Pallas kernels, on_device(): pl.pallas_call(functools.partial(step_kernel, pts, rows, ytiles, count),...  40.9 us
    add x1, other arithmetic, on_device(): new_displacement = displacement + TIME_STEP * new_velocity  1.59 us

profile of v3, /device:TPU:129, one launch (start us, length us, event | category | flops | bytes accessed | tf_op | source)
XLA Modules:
  0.0 43.2 jit_solution(16435535438567556798)
XLA Ops:
  0.6 0.0 copy-start
  0.6 0.0 copy-start.1
  0.7 40.9 %bond_step.1 = f32[3,4,8,256]{3,2,1,0:T(8,128)} custom-call(s32[3,32]{1,0:T(4,128)} %bitcast.1, f32[3,4,8,256]{3,2,1,0:T(8,128)} %displacement.1, f32[4,8,256]{2,1,0:T(8,128)} %stiffness.1, s32[32,4,64,256]{3,2,1,0:T(8,128)} %intact.1), custom_call_target="tpu_custom_call" | custom-call | tf_op jit(solution)/shard_map/bond_step/pallas_call | solution.py:425
  41.6 0.0 copy-done
  41.6 0.0 copy-done.1
  41.6 1.6 %multiply_add_fusion = (f32[3,4,8,256]{3,2,1,0:T(8,128)}, f32[3,4,8,256]{3,2,1,0:T(8,128)}) fusion(f32[3,4,8,256]{3,2,1,0:T(8,128)S(1)} %copy-done, f32[3,4,8,256]{3,2,1,0:T(8,128)S(1)} %copy-done.1, f32[3,4,8,256]{3,2,1,0:T(8,128)} %bond_step.1), kind=kLoop, calls=%fused_computation | loop fusion | flops 73728 | bytes 491520 | tf_op jit(solution)/shard_map/add | solution.py:452
Async XLA Ops:
  0.6 40.9 %copy-start = (f32[3,4,8,256]{3,2,1,0:T(8,128)S(1)}, f32[3,4,8,256]{3,2,1,0:T(8,128)}, u32[]{:S(2)}) copy-start(f32[3,4,8,256]{3,2,1,0:T(8,128)} %displacement.1) | copy-start | bytes 294916
  0.6 40.9 %copy-start.1 = (f32[3,4,8,256]{3,2,1,0:T(8,128)S(1)}, f32[3,4,8,256]{3,2,1,0:T(8,128)}, u32[]{:S(2)}) copy-start(f32[3,4,8,256]{3,2,1,0:T(8,128)} %param.6) | copy-start | bytes 294916
